TPU v7x, 32 devices: a whole 2x2x4 slice. The times are simulated.
32 devices in a mesh: dp: 4 (over y, core), mp: 8 (over z, x).
Axes of the slice: x: 2, y: 2, z: 4, core: 2. Of those that a mesh axis runs over, the one named last changes fastest.
Arguments:
- emb_grad: float32 [65536, 7168], P('dp', 'mp'), may hold values from -600 to 600
- mtp_grad: float32 [14336, 7168], P('dp', 'mp'), may hold values from -600 to 600
- emb_groups: int32 [64], replicated, may hold values from 0 to 31
- mtp_groups: int32 [32], replicated, may hold values from 0 to 31
- max_rms: float32 [1], replicated, may hold values from 0.5 to 2
Outputs:
- emb_clipped: bfloat16 [65536, 7168], P(('dp', 'mp'))
- mtp_clipped: bfloat16 [14336, 7168], P('dp', 'mp')
- group_rms: float32 [32], replicated
All inputs are finite; a program needn't handle non-finite values.
Results may differ from a plain program's by a relative error of at most 0.005.
Values may be sent and summed in bfloat16 or wider, within the bound.
A program may use at most 192 MiB of HBM per device.

v0:
```python
import functools

import jax
import jax.numpy as jnp
from jax import lax
from jax.experimental import pallas as pl
from jax.experimental.pallas import tpu as pltpu
from jax.sharding import PartitionSpec as P

EMB_BLK = 1024
MTP_BLK = 448
GROUPS = 32
STRIP = 64


def squares_kernel(x_ref, out_ref):
    height, width = x_ref.shape

    def step(i, total):
        x = x_ref[pl.ds(pl.multiple_of(i * STRIP, STRIP), STRIP), :]
        return total + jnp.sum((x * x).reshape(STRIP // 8, 8, width), axis=0)

    out_ref[0] = lax.fori_loop(0, height // STRIP, step, jnp.zeros((8, width), jnp.float32))


def block_squares(gradient, block_rows):
    rows, width = gradient.shape
    count = rows // block_rows
    sums = pl.pallas_call(
        squares_kernel,
        grid=(count,),
        in_specs=[pl.BlockSpec((block_rows, width), lambda i: (i, 0))],
        out_specs=pl.BlockSpec((1, 8, width), lambda i: (i, 0, 0)),
        out_shape=jax.ShapeDtypeStruct((count, 8, width), jnp.float32),
        cost_estimate=pl.CostEstimate(
            flops=2 * rows * width, bytes_accessed=4 * rows * width, transcendentals=0
        ),
    )(gradient)
    return jnp.sum(sums, axis=(1, 2))


def round_kernel(x_ref, out_ref):
    out_ref[...] = x_ref[...].astype(jnp.bfloat16)


def rounded_rows(by_owner, first, last, tile):
    pieces, _, width = by_owner.shape
    count = last - first
    start = first // tile
    size = pieces * count * width
    return pl.pallas_call(
        round_kernel,
        grid=(count // tile,),
        in_specs=[pl.BlockSpec((pieces, tile, width), lambda i: (0, start + i, 0))],
        out_specs=pl.BlockSpec((pieces, tile, width), lambda i: (0, i, 0)),
        out_shape=jax.ShapeDtypeStruct((pieces, count, width), jnp.bfloat16),
        cost_estimate=pl.CostEstimate(flops=size, bytes_accessed=6 * size, transcendentals=0),
    )(by_owner)


def scale_kernel(factor_ref, x_ref, *refs):
    out_ref = refs[-1]
    pieces, _, width = x_ref.shape
    factor = factor_ref[0]
    for j in range(pieces):
        out_ref[:, j * width : (j + 1) * width] = (
            x_ref[j].astype(jnp.float32) * factor
        ).astype(jnp.bfloat16)


def scale_rows(factor, arrived, out, first, rows, tile):
    pieces, count, width = arrived.shape
    start = first // tile
    in_specs = [
        pl.BlockSpec(memory_space=pltpu.SMEM),
        pl.BlockSpec((pieces, tile, width), lambda i: (0, i, 0)),
    ]
    operands = [factor.reshape(1), arrived]
    aliases = {}
    if out is not None:
        in_specs.append(pl.BlockSpec(memory_space=pl.ANY))
        operands.append(out)
        aliases = {2: 0}
    return pl.pallas_call(
        scale_kernel,
        grid=(count // tile,),
        in_specs=in_specs,
        out_specs=pl.BlockSpec((tile, pieces * width), lambda i: (start + i, 0)),
        out_shape=jax.ShapeDtypeStruct((rows, pieces * width), jnp.bfloat16),
        input_output_aliases=aliases,
        cost_estimate=pl.CostEstimate(
            flops=arrived.size, bytes_accessed=4 * arrived.size, transcendentals=0
        ),
    )(*operands)


def membership(labels):
    return (labels[:, None] == jnp.arange(GROUPS, dtype=jnp.int32)[None, :]).astype(jnp.float32)


def on_device(shards, pieces, emb_grad, mtp_grad, emb_groups, mtp_groups, max_rms):
    shard = lax.axis_index("dp")
    width = emb_grad.shape[1]
    model_width = width * pieces
    total_rows = (emb_grad.shape[0] + mtp_grad.shape[0]) * shards
    rows = emb_grad.shape[0] // pieces
    tile = rows // 32
    cuts = [0, rows // 8, rows - rows // 16, rows]

    def rounded(gradient, k):
        by_owner = gradient.reshape(pieces, rows, width)
        return rounded_rows(by_owner, cuts[k], cuts[k + 1], tile)

    def exchange(low):
        return lax.all_to_all(low, "mp", split_axis=0, concat_axis=0, tiled=True)

    low = rounded(emb_grad, 0)
    arrived = [exchange(low)]

    embed_count = emb_grad.shape[0] // EMB_BLK
    head_count = mtp_grad.shape[0] // MTP_BLK
    embed_labels = lax.dynamic_slice_in_dim(emb_groups, shard * embed_count, embed_count)
    head_labels = lax.dynamic_slice_in_dim(mtp_groups, shard * head_count, head_count)
    emb_later, mtp_later, low = lax.optimization_barrier((emb_grad, mtp_grad, low))
    partial_value = jnp.sum(
        block_squares(emb_later, EMB_BLK)[:, None] * membership(embed_labels), axis=0
    )
    partial_value = partial_value + jnp.sum(
        block_squares(mtp_later, MTP_BLK)[:, None] * membership(head_labels), axis=0
    )
    later = [rounded(emb_later, k) for k in range(1, len(cuts) - 1)]
    partial_value, later = lax.optimization_barrier((partial_value, later))
    group_square = lax.psum(partial_value, ("dp", "mp"))
    group_square, later = lax.optimization_barrier((group_square, later))
    arrived += [exchange(low) for low in later]

    group_size = jnp.sum(membership(emb_groups), axis=0) * jnp.float32(
        EMB_BLK * model_width
    ) + jnp.sum(membership(mtp_groups), axis=0) * jnp.float32(MTP_BLK * model_width)
    group_rms = jnp.sqrt(group_square / jnp.maximum(group_size, 1.0))
    global_norm = jnp.sqrt(jnp.sum(group_square))
    ceiling = max_rms[0] * jnp.sqrt(jnp.float32(total_rows * model_width))
    factor = ceiling / (global_norm + 1e-06)
    head_output = (mtp_grad * factor).astype(jnp.bfloat16)
    out = None
    for k, block in enumerate(arrived):
        out = scale_rows(factor, block, out, cuts[k], rows, tile)
    return (out, head_output, group_rms)


def solution(mesh):
    placed = (P("dp", "mp"), P("dp", "mp"), P(), P(), P())
    return jax.shard_map(
        functools.partial(on_device, mesh.shape["dp"], mesh.shape["mp"]),
        mesh=mesh,
        in_specs=placed,
        out_specs=(P(("dp", "mp"), None), P("dp", "mp"), P()),
        check_vma=False,
    )
```

profile of v0, /device:TPU:0, one launch (start us, length us, event | category | flops | bytes accessed | tf_op | source)
XLA Modules:
  0.0 696.5 jit_solution(9527447064666802837)
XLA Ops:
  0.6 5.4 shard_map.76
  6.0 7.3 %all-to-all-start.2 = ((bf16[8,256,896]{2,1,0:T(8,128)(2,1)}), bf16[8,256,896]{2,1,0:T(8,128)(2,1)}, u32[]{:S(2)}, u32[]{:S(2)}) async-start(bf16[8,256,896]{2,1,0:T(8,128)(2,1)} %shard_map.76), calls=%async_computation.2 | async-start | bytes 7340032 | tf_op jit(solution)/shard_map/all_to_all | solution.py:115
  13.3 22.6 %shard_map.77 = f32[16,8,896]{2,1,0:T(8,128)} custom-call(f32[16384,896]{1,0:T(8,128)} %x_ref), custom_call_target="tpu_custom_call" | custom-call | flops 29360128 | bytes 58720256 | tf_op jit(solution)/shard_map/pallas_call | solution.py:29
  35.9 0.0 copy-start.1
  35.9 0.0 copy-start.2
  35.9 1.3 reduce_sum.63
  37.1 7.9 %shard_map.78 = f32[8,8,896]{2,1,0:T(8,128)} custom-call(f32[3584,896]{1,0:T(8,128)} %x_ref.1), custom_call_target="tpu_custom_call" | custom-call | flops 6422528 | bytes 12845056 | tf_op jit(solution)/shard_map/pallas_call | solution.py:29
  45.0 1.1 reduce_sum.65
  46.1 0.0 copy-done.1
  46.1 0.1 dynamic_slice.6
  46.2 0.0 copy-done.2
  46.2 0.1 dynamic_slice.7
  46.2 0.1 select_reduce_fusion
  46.3 0.1 select_reduce_fusion.1
  46.4 3.1 shard_map.80
  49.5 31.5 %shard_map.79 = bf16[8,1664,896]{2,1,0:T(8,128)(2,1)} custom-call(f32[8,2048,896]{2,1,0:T(8,128)} %bitcast.6), custom_call_target="tpu_custom_call" | custom-call | flops 11927552 | bytes 71565312 | tf_op jit(solution)/shard_map/pallas_call | solution.py:51
  81.0 40.7 %psum.7 = f32[32]{0:T(128)S(1)} all-reduce(f32[32]{0:T(128)S(1)} %add.19), channel_id=1, replica_groups=mesh['dp'=4,'mp'=8] {'dp','mp'}, use_global_device_ids=true, to_apply=%region_4.0 | all-reduce | flops 32 | bytes 256 | tf_op jit(solution)/shard_map/psum | solution.py:133
  121.7 0.0 all-to-all-done.2.x_ref
  121.7 524.6 %all_to_all.15.x_ref = bf16[8,1664,896]{2,1,0:T(8,128)(2,1)} all-to-all(bf16[8,1664,896]{2,1,0:T(8,128)(2,1)} %shard_map.79), channel_id=1, replica_groups=mesh['dp'=4,'mp'=8] {'mp'}, dimensions={0} | all-to-all | bytes 47710208 | tf_op jit(solution)/shard_map/all_to_all | solution.py:115
  646.3 3.6 all-to-all-start
  650.5 0.1 convert_reduce_fusion.1
  650.7 0.1 convert_reduce_fusion
  650.7 1.1 fusion
  652.6 8.4 %multiply_convert_fusion = bf16[3584,896]{1,0:T(8,128)(2,1)} fusion(f32[3584,896]{1,0:T(8,128)} %x_ref.1, f32[]{:T(128)} %div.6), kind=kLoop, calls=%fused_computation | loop fusion | flops 6422528 | bytes 19267588 | tf_op jit(solution)/shard_map/convert_element_type | solution.py:144
  661.0 4.6 shard_map.81.refs_0_
  665.6 27.1 %shard_map.82.refs_0_ = bf16[2048,7168]{1,0:T(8,128)(2,1)} custom-call(f32[1]{0:T(128)} %bitcast.3.factor_ref, bf16[8,1664,896]{2,1,0:T(8,128)(2,1)} %all_to_all.15.x_ref, bf16[2048,7168]{1,0:T(8,128)(2,1)} %shard_map.81.refs_0_), custom_call_target="tpu_custom_call", output_to_operand_aliasing={{}: (2, {})} | custom-call | flops 11927552 | bytes 47710208 | tf_op jit(solution)/shard_map/pallas_call | solution.py:84
  692.7 0.0 all-to-all-done.x_ref
  692.7 0.0 copy-start
  692.7 1.3 copy-done
  694.0 2.6 shard_map.83
  (1 shorter events, 0.0 us)
Async XLA Ops:
  6.0 115.6 %all-to-all-start.2 = ((bf16[8,256,896]{2,1,0:T(8,128)(2,1)}), bf16[8,256,896]{2,1,0:T(8,128)(2,1)}, u32[]{:S(2)}, u32[]{:S(2)}) async-start(bf16[8,256,896]{2,1,0:T(8,128)(2,1)} %shard_map.76), calls=%async_computation.2 | async-start | bytes 7340032 | tf_op jit(solution)/shard_map/all_to_all | solution.py:115
  35.9 10.2 %copy-start.1 = (s32[64]{0:T(128)S(1)}, s32[64]{0:T(128)}, u32[]{:S(2)}) copy-start(s32[64]{0:T(128)} %param.7) | copy-start | bytes 772
  35.9 10.3 %copy-start.2 = (s32[32]{0:T(128)S(1)}, s32[32]{0:T(128)}, u32[]{:S(2)}) copy-start(s32[32]{0:T(128)} %param.8) | copy-start | bytes 388
  646.3 46.4 %all-to-all-start = ((bf16[8,128,896]{2,1,0:T(8,128)(2,1)}), bf16[8,128,896]{2,1,0:T(8,128)(2,1)S(1)}, u32[]{:S(2)}, u32[]{:S(2)}) async-start(bf16[8,128,896]{2,1,0:T(8,128)(2,1)} %shard_map.80), calls=%async_computation | async-start | bytes 3670016 | tf_op jit(solution)/shard_map/all_to_all | solution.py:115
  692.7 1.3 copy-start
where the time goes:
time: 698 us; the launch traced here: 697 us
  blocking collectives  565 us (81%)
  Pallas kernels  105 us (15%)
  other arithmetic  12.2 us (2%)
  starting transfers between devices  10.9 us (2%)
    all_to_all x1, blocking collectives, exchange(): return lax.all_to_all(low, 'mp', split_axis=0, concat_axis=0, tiled=True)  525 us
    psum x1, blocking collectives, on_device(): group_square = lax.psum(partial_value, ('dp', 'mp'))  40.7 us
    pallas_call x3, Pallas kernels, rounded_rows(): pl.pallas_call(round_kernel, grid=(count // tile,), in_specs=[pl.BlockSpe...  40 us
    pallas_call x3, Pallas kernels, scale_rows(): pl.pallas_call(scale_kernel, grid=(count // tile,), in_specs=in_specs, ou...  34.3 us
    pallas_call x2, Pallas kernels, block_squares(): pl.pallas_call(squares_kernel, grid=(count,), in_specs=[pl.BlockSpec((blo...  30.4 us
  transfers between devices with their start and end apart: 2, of which 0 were waited for; matrix products, arithmetic and copies ran while one was open for 2% of the time, Pallas kernels for 14%

commit v1 on v0

v1 whole, which is shorter than its diff:
```python
import functools

import jax
import jax.numpy as jnp
from jax import lax
from jax.experimental import pallas as pl
from jax.experimental.pallas import tpu as pltpu
from jax.sharding import PartitionSpec as P

EMB_BLK = 1024
MTP_BLK = 448
GROUPS = 32
STRIP = 32
SLOTS = 6
LANES = 128
MESH = pl.DeviceIdType.MESH


def partner(me, k, count):
    out, bit = 0, 1
    while bit < count:
        mine, other = (me // bit) % 2, (k // bit) % 2
        out = out + bit * (mine + other - 2 * mine * other)
        bit *= 2
    return out


def exchange_kernel(
    pieces, shards, tiles, tail_tiles,
    emb, mtp, arrived, tail_out, sums,
    low, tail, slots, head_slots, squares, mine, column_sums, shard_mine, shard_sums,
    load_sem, head_sem, send_sem, recv_sem, own_sem, tail_sem,
    stat_send, stat_recv, shard_send, shard_recv,
):
    me, shard = lax.axis_index("mp"), lax.axis_index("dp")
    _, rows, width = emb.shape
    tile = slots.shape[1]
    embed_blocks = pieces * rows // EMB_BLK
    head_blocks = mtp.shape[0] // MTP_BLK
    bulk = tiles - tail_tiles
    half = bulk // 2

    barrier = pltpu.get_barrier_semaphore()
    for k in range(1, pieces):
        pl.semaphore_signal(
            barrier, inc=1, device_id={"mp": partner(me, k, pieces)}, device_id_type=MESH
        )
    for k in range(1, shards):
        pl.semaphore_signal(
            barrier, inc=1, device_id={"dp": partner(shard, k, shards)}, device_id_type=MESH
        )

    squares[...] = jnp.zeros_like(squares)

    def stream(count, place, work, after):
        def load(i):
            piece, t = place(i)
            return pltpu.make_async_copy(
                emb.at[piece, pl.ds(pl.multiple_of(t * tile, tile), tile), :],
                slots.at[i % SLOTS],
                load_sem.at[i % SLOTS],
            )

        def prime():
            for i in range(min(SLOTS, count)):
                load(i).start()

        def run():
            @pl.loop(0, count)
            def _(i):
                load(i).wait()
                piece, t = place(i)
                block = (piece * rows + t * tile) // EMB_BLK
                target = work(i)
                slot = i % SLOTS

                def strip(j, total):
                    at = pl.multiple_of(j * STRIP, STRIP)
                    x = slots[slot, pl.ds(at, STRIP), :]
                    target(at, x.astype(jnp.bfloat16))
                    return total + jnp.sum((x * x).reshape(STRIP // 8, 8, width), axis=0)

                total = lax.fori_loop(
                    0, tile // STRIP, strip, jnp.zeros((8, width), jnp.float32)
                )
                squares[block] = squares[block] + total

                @pl.when(i + SLOTS < count)
                def _():
                    load(i + SLOTS).start()

                @pl.when(i > 0)
                def _():
                    after(i - 1)

            after(count - 1)

        return prime, run

    def send(k, t):
        at = pl.ds(pl.multiple_of(t * tile, tile), tile)
        return pltpu.make_async_remote_copy(
            src_ref=low.at[k, at, :],
            dst_ref=arrived.at[me, at, :],
            send_sem=send_sem.at[k],
            recv_sem=recv_sem.at[k],
            device_id={"mp": partner(me, k, pieces)},
            device_id_type=MESH,
        )

    others = pieces - 1

    def group_of(i):
        return 1 + (i + 1) % others

    def store_low(k, t):
        def target(at, value):
            low[k, pl.ds(pl.multiple_of(t * tile + at, STRIP), STRIP), :] = value

        return target

    first_prime, first_run = stream(
        others,
        lambda i: (partner(me, group_of(i), pieces), 0),
        lambda i: store_low(group_of(i), 0),
        lambda i: send(group_of(i), 0).start(),
    )
    first_prime()
    pl.semaphore_wait(barrier, pieces - 1 + shards - 1)
    first_run()

    rest = bulk - 1

    def rest_after(i):
        k, t = group_of(i // rest), 1 + i % rest

        @pl.when((k < pieces // 2) | (t < half))
        def _():
            send(k, t).start()

    rest_prime, rest_run = stream(
        others * rest,
        lambda i: (partner(me, group_of(i // rest), pieces), 1 + i % rest),
        lambda i: store_low(group_of(i // rest), 1 + i % rest),
        rest_after,
    )
    rest_prime()
    rest_run()

    def own_copy(t):
        at = pl.ds(pl.multiple_of(t * tile, tile), tile)
        return pltpu.make_async_copy(low.at[0, at, :], arrived.at[me, at, :], own_sem)

    own_prime, own_run = stream(
        bulk, lambda i: (me, i), lambda i: store_low(0, i), lambda i: own_copy(i).start()
    )
    own_prime()
    own_run()

    def store_tail(i):
        def target(at, value):
            row = pl.multiple_of((i % tail_tiles) * tile + at, STRIP)
            tail[i // tail_tiles, pl.ds(row, STRIP), :] = value

        return target

    def tail_copy(i):
        at = pl.ds(pl.multiple_of((i % tail_tiles) * tile, tile), tile)
        piece = i // tail_tiles
        return pltpu.make_async_copy(
            tail.at[piece, at, :], tail_out.at[piece, at, :], tail_sem
        )

    tail_prime, tail_run = stream(
        pieces * tail_tiles,
        lambda i: (i // tail_tiles, bulk + i % tail_tiles),
        store_tail,
        lambda i: tail_copy(i).start(),
    )
    tail_prime()
    tail_run()

    def head_load(b):
        return pltpu.make_async_copy(
            mtp.at[pl.ds(pl.multiple_of(b * MTP_BLK, MTP_BLK), MTP_BLK), :],
            head_slots.at[b % 2],
            head_sem.at[b % 2],
        )

    for b in range(min(2, head_blocks)):
        head_load(b).start()

    @pl.loop(0, head_blocks)
    def _(b):
        head_load(b).wait()

        def strip(j, total):
            x = head_slots[b % 2, pl.ds(pl.multiple_of(j * STRIP, STRIP), STRIP), :]
            return total + jnp.sum((x * x).reshape(STRIP // 8, 8, width), axis=0)

        squares[embed_blocks + b] = lax.fori_loop(
            0, MTP_BLK // STRIP, strip, jnp.zeros((8, width), jnp.float32)
        )

        @pl.when(b + 2 < head_blocks)
        def _():
            head_load(b + 2).start()

    lane = lax.broadcasted_iota(jnp.int32, (8, LANES), 0) * LANES + lax.broadcasted_iota(
        jnp.int32, (8, LANES), 1
    )

    def pack(b, total):
        return jnp.where(lane == b, jnp.sum(squares[b]), total)

    packed = lax.fori_loop(
        0, embed_blocks + head_blocks, pack, jnp.zeros((8, LANES), jnp.float32)
    )
    mine[...] = packed
    column_sums[me] = packed

    def far_sends(low_tile, high_tile):
        span = high_tile - low_tile

        @pl.loop(0, (pieces - pieces // 2) * span)
        def _(i):
            send(pieces // 2 + i // span, low_tile + i % span).start()

    split = half + (bulk - half) // 2
    far_sends(half, split)

    def stat_copy(k):
        return pltpu.make_async_remote_copy(
            src_ref=mine,
            dst_ref=column_sums.at[me],
            send_sem=stat_send.at[k],
            recv_sem=stat_recv.at[k],
            device_id={"mp": partner(me, k, pieces)},
            device_id_type=MESH,
        )

    for k in range(1, pieces):
        stat_copy(k).start()
    far_sends(split, bulk)
    for k in range(1, pieces):
        stat_copy(k).wait()
    packed = jnp.sum(column_sums[...], axis=0)
    shard_mine[...] = packed
    shard_sums[shard] = packed

    def whole_copy(k):
        at = pl.ds(0, bulk * tile)
        return pltpu.make_async_remote_copy(
            src_ref=low.at[k, at, :],
            dst_ref=arrived.at[me, at, :],
            send_sem=send_sem.at[k],
            recv_sem=recv_sem.at[k],
            device_id={"mp": partner(me, k, pieces)},
            device_id_type=MESH,
        )

    whole_copy(1).wait_send()

    def shard_copy(k):
        return pltpu.make_async_remote_copy(
            src_ref=shard_mine,
            dst_ref=shard_sums.at[shard],
            send_sem=shard_send.at[k],
            recv_sem=shard_recv.at[k],
            device_id={"dp": partner(shard, k, shards)},
            device_id_type=MESH,
        )

    for k in range(1, shards):
        shard_copy(k).start()
    for k in range(1, shards):
        shard_copy(k).wait()
    sums[...] = shard_sums[...]

    at = pl.ds(0, bulk * tile)
    pltpu.make_async_copy(low.at[0, at, :], arrived.at[me, at, :], own_sem).wait()
    pltpu.make_async_copy(tail, tail_out, tail_sem).wait()
    whole_copy(1).wait_recv()
    for k in range(2, pieces):
        whole_copy(k).wait()


def round_and_exchange(by_owner, mtp, shards, tiles, tail_tiles):
    pieces, rows, width = by_owner.shape
    tile = rows // tiles
    bulk_rows, tail_rows = (tiles - tail_tiles) * tile, tail_tiles * tile
    blocks = pieces * rows // EMB_BLK + mtp.shape[0] // MTP_BLK
    return pl.pallas_call(
        functools.partial(exchange_kernel, pieces, shards, tiles, tail_tiles),
        in_specs=[pl.BlockSpec(memory_space=pl.ANY)] * 2,
        out_specs=[
            pl.BlockSpec(memory_space=pl.ANY),
            pl.BlockSpec(memory_space=pl.ANY),
            pl.BlockSpec(memory_space=pltpu.VMEM),
        ],
        out_shape=[
            jax.ShapeDtypeStruct((pieces, bulk_rows, width), jnp.bfloat16),
            jax.ShapeDtypeStruct((pieces, tail_rows, width), jnp.bfloat16),
            jax.ShapeDtypeStruct((shards, 8, LANES), jnp.float32),
        ],
        scratch_shapes=[
            pltpu.VMEM((pieces, bulk_rows, width), jnp.bfloat16),
            pltpu.VMEM((pieces, tail_rows, width), jnp.bfloat16),
            pltpu.VMEM((SLOTS, tile, width), jnp.float32),
            pltpu.VMEM((2, MTP_BLK, width), jnp.float32),
            pltpu.VMEM((blocks, 8, width), jnp.float32),
            pltpu.VMEM((8, LANES), jnp.float32),
            pltpu.VMEM((pieces, 8, LANES), jnp.float32),
            pltpu.VMEM((8, LANES), jnp.float32),
            pltpu.VMEM((shards, 8, LANES), jnp.float32),
            pltpu.SemaphoreType.DMA((SLOTS,)),
            pltpu.SemaphoreType.DMA((2,)),
            pltpu.SemaphoreType.DMA((pieces,)),
            pltpu.SemaphoreType.DMA((pieces,)),
            pltpu.SemaphoreType.DMA,
            pltpu.SemaphoreType.DMA,
            pltpu.SemaphoreType.DMA((pieces,)),
            pltpu.SemaphoreType.DMA((pieces,)),
            pltpu.SemaphoreType.DMA((shards,)),
            pltpu.SemaphoreType.DMA((shards,)),
        ],
        compiler_params=pltpu.CompilerParams(
            collective_id=0, has_side_effects=True, vmem_limit_bytes=60_000_000
        ),
        cost_estimate=pl.CostEstimate(
            flops=3 * by_owner.size, bytes_accessed=8 * by_owner.size, transcendentals=0
        ),
    )(by_owner, mtp)


def scale_kernel(factor_ref, x_ref, *refs):
    out_ref = refs[-1]
    pieces, _, width = x_ref.shape
    factor = factor_ref[0]
    for j in range(pieces):
        out_ref[:, j * width : (j + 1) * width] = (
            x_ref[j].astype(jnp.float32) * factor
        ).astype(jnp.bfloat16)


def scale_rows(factor, arrived, out, first, rows, tile):
    pieces, count, width = arrived.shape
    start = first // tile
    in_specs = [
        pl.BlockSpec(memory_space=pltpu.SMEM),
        pl.BlockSpec((pieces, tile, width), lambda i: (0, i, 0)),
    ]
    operands = [factor.reshape(1), arrived]
    aliases = {}
    if out is not None:
        in_specs.append(pl.BlockSpec(memory_space=pl.ANY))
        operands.append(out)
        aliases = {2: 0}
    return pl.pallas_call(
        scale_kernel,
        grid=(count // tile,),
        in_specs=in_specs,
        out_specs=pl.BlockSpec((tile, pieces * width), lambda i: (start + i, 0)),
        out_shape=jax.ShapeDtypeStruct((rows, pieces * width), jnp.bfloat16),
        input_output_aliases=aliases,
        cost_estimate=pl.CostEstimate(
            flops=arrived.size, bytes_accessed=4 * arrived.size, transcendentals=0
        ),
    )(*operands)


def membership(labels):
    return (labels[:, None] == jnp.arange(GROUPS, dtype=jnp.int32)[None, :]).astype(jnp.float32)


def on_device(shards, pieces, emb_grad, mtp_grad, emb_groups, mtp_groups, max_rms):
    width = emb_grad.shape[1]
    model_width = width * pieces
    total_rows = (emb_grad.shape[0] + mtp_grad.shape[0]) * shards
    rows = emb_grad.shape[0] // pieces
    tiles, tail_tiles = 16, 1
    tile = rows // tiles
    bulk_rows = (tiles - tail_tiles) * tile

    by_owner = emb_grad.reshape(pieces, rows, width)
    arrived, tail, sums = round_and_exchange(by_owner, mtp_grad, shards, tiles, tail_tiles)
    tail_arrived = lax.all_to_all(tail, "mp", split_axis=0, concat_axis=0, tiled=True)

    embed_count = emb_grad.shape[0] // EMB_BLK
    head_count = mtp_grad.shape[0] // MTP_BLK
    flat = sums.reshape(shards, 8 * LANES)
    embed_squares = flat[:, :embed_count].reshape(-1)
    head_squares = flat[:, embed_count : embed_count + head_count].reshape(-1)
    embed_member, head_member = membership(emb_groups), membership(mtp_groups)
    group_square = jnp.sum(embed_squares[:, None] * embed_member, axis=0) + jnp.sum(
        head_squares[:, None] * head_member, axis=0
    )
    group_size = jnp.sum(embed_member, axis=0) * jnp.float32(
        EMB_BLK * model_width
    ) + jnp.sum(head_member, axis=0) * jnp.float32(MTP_BLK * model_width)
    group_rms = jnp.sqrt(group_square / jnp.maximum(group_size, 1.0))
    global_norm = jnp.sqrt(jnp.sum(group_square))
    ceiling = max_rms[0] * jnp.sqrt(jnp.float32(total_rows * model_width))
    factor = ceiling / (global_norm + 1e-06)
    out = scale_rows(factor, arrived, None, 0, rows, tile)
    head_output = (mtp_grad * factor).astype(jnp.bfloat16)
    out = scale_rows(factor, tail_arrived, out, bulk_rows, rows, tile)
    return (out, head_output, group_rms)


def solution(mesh):
    placed = (P("dp", "mp"), P("dp", "mp"), P(), P(), P())
    return jax.shard_map(
        functools.partial(on_device, mesh.shape["dp"], mesh.shape["mp"]),
        mesh=mesh,
        in_specs=placed,
        out_specs=(P(("dp", "mp"), None), P("dp", "mp"), P()),
        check_vma=False,
    )
```

time: 698 us -> 678 us (0.971)
  blocking collectives: 565 us -> 0 us
  Pallas kernels: 105 us -> 618 us
  starting transfers between devices: 10.9 us -> 41.1 us
    all_to_all x1 -> x0, blocking collectives: 525 us -> none  [exchange(): return lax.all_to_all(low, 'mp', split_axis=0, concat_axis=0, tiled=True)]
    pallas_call x5 -> x1, Pallas kernels: 70.4 us -> 589 us  [round_and_exchange(): pl.pallas_call(functools.partial(exchange_kernel, pieces, shards, tiles,...]
    psum x1 -> x0, blocking collectives: 40.7 us -> none  [on_device(): group_square = lax.psum(partial_value, ('dp', 'mp'))]
    all_to_all x2 -> x1, starting transfers between devices: 10.9 us -> 41.1 us  [on_device(): lax.all_to_all(tail, 'mp', split_axis=0, concat_axis=0, tiled=True)]
    pallas_call x3 -> x2, Pallas kernels: 34.3 us -> 28.4 us  [scale_rows(): pl.pallas_call(scale_kernel, grid=(count // tile,), in_specs=in_specs, ou...]
  transfers between devices with their start and end apart: 2 -> 1, of which waited for: 0 -> 1; matrix products, arithmetic and copies ran while one was open for 2% -> 2% of each run, Pallas kernels for 14% -> 4%
where the time goes in v1:
time: 678 us; the launch traced here: 677 us
  Pallas kernels  618 us (91%)
  starting transfers between devices  41.1 us (6%)
  other arithmetic  9.72 us (1%)
    pallas_call x1, Pallas kernels, round_and_exchange(): pl.pallas_call(functools.partial(exchange_kernel, pieces, shards, tiles,...  589 us
    all_to_all x1, starting transfers between devices, on_device(): lax.all_to_all(tail, 'mp', split_axis=0, concat_axis=0, tiled=True)  41.1 us
    pallas_call x2, Pallas kernels, scale_rows(): pl.pallas_call(scale_kernel, grid=(count // tile,), in_specs=in_specs, ou...  28.4 us
  transfers between devices with their start and end apart: 1, of which 1 were waited for; matrix products, arithmetic and copies ran while one was open for 2% of the time, Pallas kernels for 4%

profile of v1, /device:TPU:0, one launch (start us, length us, event | category | flops | bytes accessed | tf_op | source)
XLA Modules:
  0.0 677.1 jit_solution(7426270887830623022)
XLA Ops:
  0.6 0.0 copy-start.1
  0.6 0.0 copy-start.2
  0.7 589.3 %shard_map.76 = (bf16[8,1920,896]{2,1,0:T(8,128)(2,1)}, bf16[8,128,896]{2,1,0:T(8,128)(2,1)}, f32[4,8,128]{2,1,0:T(8,128)}) custom-call(f32[8,2048,896]{2,1,0:T(8,128)} %bitcast.7, f32[3584,896]{1,0:T(8,128)} %mtp.1), custom_call_target="tpu_custom_call" | custom-call | flops 44040192 | bytes 117440512 | tf_op jit(solution)/shard_map/pallas_call | solution.py:293
  589.9 41.1 %all-to-all-start = ((bf16[8,128,896]{2,1,0:T(8,128)(2,1)}), bf16[8,128,896]{2,1,0:T(8,128)(2,1)S(1)}, u32[]{:S(2)}, u32[]{:S(2)}) async-start(bf16[8,128,896]{2,1,0:T(8,128)(2,1)} %get-tuple-element.7), calls=%async_computation | async-start | bytes 3670016 | tf_op jit(solution)/shard_map/all_to_all | solution.py:387
  631.0 0.7 copy.11
  631.7 0.1 slice.9
  632.4 0.1 mul.46
  632.5 0.1 mul.49
  632.6 0.0 copy-done.1
  632.6 0.1 convert_reduce_fusion.1
  632.7 0.0 copy-done.2
  632.7 0.1 convert_reduce_fusion
  632.8 1.1 fusion
  634.7 25.4 %shard_map.77.refs_0_ = bf16[2048,7168]{1,0:T(8,128)(2,1)} custom-call(f32[1]{0:T(128)} %bitcast.2.factor_ref, bf16[8,1920,896]{2,1,0:T(8,128)(2,1)} %get-tuple-element.8.x_ref), custom_call_target="tpu_custom_call" | custom-call | flops 13762560 | bytes 55050240 | tf_op jit(solution)/shard_map/pallas_call | solution.py:359
  660.1 8.4 %multiply_convert_fusion = bf16[3584,896]{1,0:T(8,128)(2,1)} fusion(f32[3584,896]{1,0:T(8,128)} %mtp.1, f32[]{:T(128)} %div.6), kind=kLoop, calls=%fused_computation | loop fusion | flops 6422528 | bytes 19267588 | tf_op jit(solution)/shard_map/convert_element_type | solution.py:406
  668.5 4.4 all-to-all-done.x_ref
  672.9 0.0 copy-start
  672.9 1.3 copy-done
  674.1 3.0 shard_map.78
  (1 shorter events, 0.0 us)
Async XLA Ops:
  0.6 632.0 %copy-start.1 = (s32[64]{0:T(128)S(1)}, s32[64]{0:T(128)}, u32[]{:S(2)}) copy-start(s32[64]{0:T(128)} %param.7) | copy-start | bytes 772
  0.6 632.1 %copy-start.2 = (s32[32]{0:T(128)S(1)}, s32[32]{0:T(128)}, u32[]{:S(2)}) copy-start(s32[32]{0:T(128)} %param.8) | copy-start | bytes 388
  589.9 82.9 %all-to-all-start = ((bf16[8,128,896]{2,1,0:T(8,128)(2,1)}), bf16[8,128,896]{2,1,0:T(8,128)(2,1)S(1)}, u32[]{:S(2)}, u32[]{:S(2)}) async-start(bf16[8,128,896]{2,1,0:T(8,128)(2,1)} %get-tuple-element.7), calls=%async_computation | async-start | bytes 3670016 | tf_op jit(solution)/shard_map/all_to_all | solution.py:387
  672.9 1.3 copy-start

commit v2 on v1

--- a/solution.py
+++ b/solution.py
@@ -12,6 +12,7 @@
 GROUPS = 32
 STRIP = 32
 SLOTS = 6
+LEAD = 2
 LANES = 128
 MESH = pl.DeviceIdType.MESH
 
@@ -38,7 +39,6 @@
     embed_blocks = pieces * rows // EMB_BLK
     head_blocks = mtp.shape[0] // MTP_BLK
     bulk = tiles - tail_tiles
-    half = bulk // 2
 
     barrier = pltpu.get_barrier_semaphore()
     for k in range(1, pieces):
@@ -52,7 +52,7 @@
 
     squares[...] = jnp.zeros_like(squares)
 
-    def stream(count, place, work, after):
+    def stream(count, place, store, after):
         def load(i):
             piece, t = place(i)
             return pltpu.make_async_copy(
@@ -71,13 +71,12 @@
                 load(i).wait()
                 piece, t = place(i)
                 block = (piece * rows + t * tile) // EMB_BLK
-                target = work(i)
                 slot = i % SLOTS
 
                 def strip(j, total):
                     at = pl.multiple_of(j * STRIP, STRIP)
                     x = slots[slot, pl.ds(at, STRIP), :]
-                    target(at, x.astype(jnp.bfloat16))
+                    store(i, at, x.astype(jnp.bfloat16))
                     return total + jnp.sum((x * x).reshape(STRIP // 8, 8, width), axis=0)
 
                 total = lax.fori_loop(
@@ -97,8 +96,11 @@
 
         return prime, run
 
-    def send(k, t):
-        at = pl.ds(pl.multiple_of(t * tile, tile), tile)
+    def store_low(k, t, at, value):
+        low[k, pl.ds(pl.multiple_of(t * tile + at, STRIP), STRIP), :] = value
+
+    def send(k, start, count):
+        at = pl.ds(pl.multiple_of(start * tile, tile), count * tile)
         return pltpu.make_async_remote_copy(
             src_ref=low.at[k, at, :],
             dst_ref=arrived.at[me, at, :],
@@ -108,77 +110,73 @@
             device_id_type=MESH,
         )
 
-    others = pieces - 1
-
-    def group_of(i):
-        return 1 + (i + 1) % others
-
-    def store_low(k, t):
-        def target(at, value):
-            low[k, pl.ds(pl.multiple_of(t * tile + at, STRIP), STRIP), :] = value
-
-        return target
-
-    first_prime, first_run = stream(
-        others,
-        lambda i: (partner(me, group_of(i), pieces), 0),
-        lambda i: store_low(group_of(i), 0),
-        lambda i: send(group_of(i), 0).start(),
-    )
-    first_prime()
+    middle = pieces // 2
+    near = list(range(2, middle))
+    early = list(range(pieces - 1, middle + middle // 2 - 1, -1))
+    late = list(range(middle, middle + middle // 2))
+    lead = min(LEAD, bulk - 1)
+    paired = min(len(near), len(early))
+
+    def lead_piece(i):
+        pair = (i // 2) % paired
+        return (1 - i % 2) * (2 + pair) + (i % 2) * (pieces - 1 - pair)
+
+    def lead_tile(i):
+        return i // (2 * paired)
+
+    prime, run = stream(
+        2 * paired * lead,
+        lambda i: (partner(me, lead_piece(i), pieces), lead_tile(i)),
+        lambda i, at, value: store_low(lead_piece(i), lead_tile(i), at, value),
+        lambda i: send(lead_piece(i), lead_tile(i), 1).start(),
+    )
+    prime()
     pl.semaphore_wait(barrier, pieces - 1 + shards - 1)
-    first_run()
-
-    rest = bulk - 1
-
-    def rest_after(i):
-        k, t = group_of(i // rest), 1 + i % rest
-
-        @pl.when((k < pieces // 2) | (t < half))
-        def _():
-            send(k, t).start()
-
-    rest_prime, rest_run = stream(
-        others * rest,
-        lambda i: (partner(me, group_of(i // rest), pieces), 1 + i % rest),
-        lambda i: store_low(group_of(i // rest), 1 + i % rest),
-        rest_after,
-    )
-    rest_prime()
-    rest_run()
-
-    def own_copy(t):
-        at = pl.ds(pl.multiple_of(t * tile, tile), tile)
-        return pltpu.make_async_copy(low.at[0, at, :], arrived.at[me, at, :], own_sem)
-
-    own_prime, own_run = stream(
-        bulk, lambda i: (me, i), lambda i: store_low(0, i), lambda i: own_copy(i).start()
-    )
-    own_prime()
-    own_run()
-
-    def store_tail(i):
-        def target(at, value):
-            row = pl.multiple_of((i % tail_tiles) * tile + at, STRIP)
-            tail[i // tail_tiles, pl.ds(row, STRIP), :] = value
-
-        return target
-
-    def tail_copy(i):
-        at = pl.ds(pl.multiple_of((i % tail_tiles) * tile, tile), tile)
-        piece = i // tail_tiles
-        return pltpu.make_async_copy(
-            tail.at[piece, at, :], tail_out.at[piece, at, :], tail_sem
-        )
-
-    tail_prime, tail_run = stream(
+    run()
+
+    waiting = []
+    for k in near + early + late + [1]:
+        started = lead if k in near[:paired] + early[:paired] else 0
+        prime, run = stream(
+            bulk - started,
+            lambda i: (partner(me, k, pieces), started + i),
+            lambda i, at, value: store_low(k, started + i, at, value),
+            lambda i: None,
+        )
+        prime()
+        run()
+        for copy in waiting:
+            copy.start()
+        waiting = [send(k, started, bulk - started)] if k in near + early else []
+    first_late = late[0]
+    half = bulk // 2
+
+    own_at = pl.ds(0, bulk * tile)
+    own_copy = pltpu.make_async_copy(low.at[0, own_at, :], arrived.at[me, own_at, :], own_sem)
+    prime, run = stream(
+        bulk,
+        lambda i: (me, i),
+        lambda i, at, value: store_low(0, i, at, value),
+        lambda i: None,
+    )
+    prime()
+    run()
+    send(first_late, 0, half).start()
+
+    def store_tail(i, at, value):
+        row = pl.multiple_of((i % tail_tiles) * tile + at, STRIP)
+        tail[i // tail_tiles, pl.ds(row, STRIP), :] = value
+
+    tail_copy = pltpu.make_async_copy(tail, tail_out, tail_sem)
+    prime, run = stream(
         pieces * tail_tiles,
         lambda i: (i // tail_tiles, bulk + i % tail_tiles),
         store_tail,
-        lambda i: tail_copy(i).start(),
-    )
-    tail_prime()
-    tail_run()
+        lambda i: None,
+    )
+    prime()
+    run()
+    own_copy.start()
 
     def head_load(b):
         return pltpu.make_async_copy(
@@ -219,15 +217,11 @@
     mine[...] = packed
     column_sums[me] = packed
 
-    def far_sends(low_tile, high_tile):
-        span = high_tile - low_tile
-
-        @pl.loop(0, (pieces - pieces // 2) * span)
-        def _(i):
-            send(pieces // 2 + i // span, low_tile + i % span).start()
-
-    split = half + (bulk - half) // 2
-    far_sends(half, split)
+    tail_copy.start()
+
+    for k in near:
+        send(k, 0, bulk).wait_send()
+    send(1, 0, bulk).start()
 
     def stat_copy(k):
         return pltpu.make_async_remote_copy(
@@ -241,25 +235,14 @@
 
     for k in range(1, pieces):
         stat_copy(k).start()
-    far_sends(split, bulk)
+    send(first_late, half, bulk - half).start()
+    for k in late[1:]:
+        send(k, 0, bulk).start()
     for k in range(1, pieces):
         stat_copy(k).wait()
     packed = jnp.sum(column_sums[...], axis=0)
     shard_mine[...] = packed
     shard_sums[shard] = packed
-
-    def whole_copy(k):
-        at = pl.ds(0, bulk * tile)
-        return pltpu.make_async_remote_copy(
-            src_ref=low.at[k, at, :],
-            dst_ref=arrived.at[me, at, :],
-            send_sem=send_sem.at[k],
-            recv_sem=recv_sem.at[k],
-            device_id={"mp": partner(me, k, pieces)},
-            device_id_type=MESH,
-        )
-
-    whole_copy(1).wait_send()
 
     def shard_copy(k):
         return pltpu.make_async_remote_copy(
@@ -277,12 +260,12 @@
         shard_copy(k).wait()
     sums[...] = shard_sums[...]
 
-    at = pl.ds(0, bulk * tile)
-    pltpu.make_async_copy(low.at[0, at, :], arrived.at[me, at, :], own_sem).wait()
-    pltpu.make_async_copy(tail, tail_out, tail_sem).wait()
-    whole_copy(1).wait_recv()
-    for k in range(2, pieces):
-        whole_copy(k).wait()
+    own_copy.wait()
+    tail_copy.wait()
+    for k in range(1, pieces):
+        if k not in near:
+            send(k, 0, bulk).wait_send()
+        send(k, 0, bulk).wait_recv()
 
 
 def round_and_exchange(by_owner, mtp, shards, tiles, tail_tiles):

time: 678 us -> 652 us (0.962)
  starting transfers between devices: 41.1 us -> 3.99 us
  Pallas kernels: 618 us -> 628 us
    all_to_all x1, starting transfers between devices: 41.1 us -> 3.99 us  [on_device(): lax.all_to_all(tail, 'mp', split_axis=0, concat_axis=0, tiled=True)]
    pallas_call x1, Pallas kernels: 589 us -> 600 us  [round_and_exchange(): pl.pallas_call(functools.partial(exchange_kernel, pieces, shards, tiles,...]
where the time goes in v2:
time: 652 us; the launch traced here: 651 us
  Pallas kernels  628 us (96%)
  other arithmetic  9.72 us (1%)
    pallas_call x1, Pallas kernels, round_and_exchange(): pl.pallas_call(functools.partial(exchange_kernel, pieces, shards, tiles,...  600 us
    pallas_call x2, Pallas kernels, scale_rows(): pl.pallas_call(scale_kernel, grid=(count // tile,), in_specs=in_specs, ou...  28.4 us
  transfers between devices with their start and end apart: 1, of which 1 were waited for; matrix products, arithmetic and copies ran while one was open for 2% of the time, Pallas kernels for 4%

profile of v2, /device:TPU:0, one launch (start us, length us, event | category | flops | bytes accessed | tf_op | source)
XLA Modules:
  0.0 650.9 jit_solution(15312004137292082421)
XLA Ops:
  0.6 0.0 copy-start.1
  0.6 0.0 copy-start.2
  0.7 599.8 %shard_map.76 = (bf16[8,1920,896]{2,1,0:T(8,128)(2,1)}, bf16[8,128,896]{2,1,0:T(8,128)(2,1)}, f32[4,8,128]{2,1,0:T(8,128)}) custom-call(f32[8,2048,896]{2,1,0:T(8,128)} %bitcast.7, f32[3584,896]{1,0:T(8,128)} %mtp.1), custom_call_target="tpu_custom_call" | custom-call | flops 44040192 | bytes 117440512 | tf_op jit(solution)/shard_map/pallas_call | solution.py:276
  600.5 4.0 all-to-all-start
  604.4 0.7 copy.11
  605.2 0.1 slice.9
  605.9 0.1 mul.46
  606.0 0.1 mul.49
  606.1 0.0 copy-done.1
  606.1 0.1 convert_reduce_fusion.1
  606.2 0.0 copy-done.2
  606.2 0.1 convert_reduce_fusion
  606.3 1.1 fusion
  608.1 25.4 %shard_map.77.refs_0_ = bf16[2048,7168]{1,0:T(8,128)(2,1)} custom-call(f32[1]{0:T(128)} %bitcast.2.factor_ref, bf16[8,1920,896]{2,1,0:T(8,128)(2,1)} %get-tuple-element.8.x_ref), custom_call_target="tpu_custom_call" | custom-call | flops 13762560 | bytes 55050240 | tf_op jit(solution)/shard_map/pallas_call | solution.py:342
  633.5 8.4 %multiply_convert_fusion = bf16[3584,896]{1,0:T(8,128)(2,1)} fusion(f32[3584,896]{1,0:T(8,128)} %mtp.1, f32[]{:T(128)} %div.6), kind=kLoop, calls=%fused_computation | loop fusion | flops 6422528 | bytes 19267588 | tf_op jit(solution)/shard_map/convert_element_type | solution.py:389
  641.9 4.7 all-to-all-done.x_ref
  646.6 0.0 copy-start
  646.6 1.3 copy-done
  647.8 3.0 shard_map.78
  (1 shorter events, 0.0 us)
Async XLA Ops:
  0.6 605.4 %copy-start.1 = (s32[64]{0:T(128)S(1)}, s32[64]{0:T(128)}, u32[]{:S(2)}) copy-start(s32[64]{0:T(128)} %param.7) | copy-start | bytes 772
  0.6 605.5 %copy-start.2 = (s32[32]{0:T(128)S(1)}, s32[32]{0:T(128)}, u32[]{:S(2)}) copy-start(s32[32]{0:T(128)} %param.8) | copy-start | bytes 388
  600.5 46.1 %all-to-all-start = ((bf16[8,128,896]{2,1,0:T(8,128)(2,1)}), bf16[8,128,896]{2,1,0:T(8,128)(2,1)S(1)}, u32[]{:S(2)}, u32[]{:S(2)}) async-start(bf16[8,128,896]{2,1,0:T(8,128)(2,1)} %get-tuple-element.7), calls=%async_computation | async-start | bytes 3670016 | tf_op jit(solution)/shard_map/all_to_all | solution.py:370
  646.6 1.3 copy-start

commit v3 on v2

--- a/solution.py
+++ b/solution.py
@@ -50,8 +50,6 @@
             barrier, inc=1, device_id={"dp": partner(shard, k, shards)}, device_id_type=MESH
         )
 
-    squares[...] = jnp.zeros_like(squares)
-
     def stream(count, place, store, after):
         def load(i):
             piece, t = place(i)
@@ -113,7 +111,7 @@
     middle = pieces // 2
     near = list(range(2, middle))
     early = list(range(pieces - 1, middle + middle // 2 - 1, -1))
-    late = list(range(middle, middle + middle // 2))
+    late = list(range(middle + middle // 2 - 1, middle - 1, -1))
     lead = min(LEAD, bulk - 1)
     paired = min(len(near), len(early))
 
@@ -128,11 +126,15 @@
         2 * paired * lead,
         lambda i: (partner(me, lead_piece(i), pieces), lead_tile(i)),
         lambda i, at, value: store_low(lead_piece(i), lead_tile(i), at, value),
-        lambda i: send(lead_piece(i), lead_tile(i), 1).start(),
+        lambda i: None,
     )
     prime()
+    squares[...] = jnp.zeros_like(squares)
+    run()
     pl.semaphore_wait(barrier, pieces - 1 + shards - 1)
-    run()
+    for pair in range(paired):
+        send(near[pair], 0, lead).start()
+        send(early[pair], 0, lead).start()
 
     waiting = []
     for k in near + early + late + [1]:
@@ -316,8 +318,7 @@
     )(by_owner, mtp)
 
 
-def scale_kernel(factor_ref, x_ref, *refs):
-    out_ref = refs[-1]
+def scale_kernel(factor_ref, x_ref, out_ref):
     pieces, _, width = x_ref.shape
     factor = factor_ref[0]
     for j in range(pieces):
@@ -326,30 +327,52 @@
         ).astype(jnp.bfloat16)
 
 
-def scale_rows(factor, arrived, out, first, rows, tile):
+def scale_rows(factor, arrived, rows, tile):
     pieces, count, width = arrived.shape
-    start = first // tile
-    in_specs = [
-        pl.BlockSpec(memory_space=pltpu.SMEM),
-        pl.BlockSpec((pieces, tile, width), lambda i: (0, i, 0)),
-    ]
-    operands = [factor.reshape(1), arrived]
-    aliases = {}
-    if out is not None:
-        in_specs.append(pl.BlockSpec(memory_space=pl.ANY))
-        operands.append(out)
-        aliases = {2: 0}
     return pl.pallas_call(
         scale_kernel,
         grid=(count // tile,),
-        in_specs=in_specs,
-        out_specs=pl.BlockSpec((tile, pieces * width), lambda i: (start + i, 0)),
+        in_specs=[
+            pl.BlockSpec(memory_space=pltpu.SMEM),
+            pl.BlockSpec((pieces, tile, width), lambda i: (0, i, 0)),
+        ],
+        out_specs=pl.BlockSpec((tile, pieces * width), lambda i: (i, 0)),
         out_shape=jax.ShapeDtypeStruct((rows, pieces * width), jnp.bfloat16),
-        input_output_aliases=aliases,
         cost_estimate=pl.CostEstimate(
             flops=arrived.size, bytes_accessed=4 * arrived.size, transcendentals=0
         ),
-    )(*operands)
+    )(factor.reshape(1), arrived)
+
+
+def scale_tail_kernel(step, factor_ref, x_ref, _, out_ref):
+    pieces, _, width = x_ref.shape
+    factor = factor_ref[0]
+    at = pl.ds(pl.multiple_of(pl.program_id(0) * step, step), step)
+    for j in range(pieces):
+        out_ref[:, j * width : (j + 1) * width] = (
+            x_ref[j, at, :].astype(jnp.float32) * factor
+        ).astype(jnp.bfloat16)
+
+
+def scale_tail(factor, arrived, out, step):
+    pieces, count, width = arrived.shape
+    start = (out.shape[0] - count) // step
+    return pl.pallas_call(
+        functools.partial(scale_tail_kernel, step),
+        grid=(count // step,),
+        in_specs=[
+            pl.BlockSpec(memory_space=pltpu.SMEM),
+            pl.BlockSpec(memory_space=pltpu.VMEM),
+            pl.BlockSpec(memory_space=pl.ANY),
+        ],
+        out_specs=pl.BlockSpec((step, pieces * width), lambda i: (start + i, 0)),
+        out_shape=jax.ShapeDtypeStruct(out.shape, jnp.bfloat16),
+        input_output_aliases={2: 0},
+        compiler_params=pltpu.CompilerParams(vmem_limit_bytes=16 * step * pieces * width),
+        cost_estimate=pl.CostEstimate(
+            flops=arrived.size, bytes_accessed=4 * arrived.size, transcendentals=0
+        ),
+    )(factor.reshape(1), arrived, out)
 
 
 def membership(labels):
@@ -363,7 +386,6 @@
     rows = emb_grad.shape[0] // pieces
     tiles, tail_tiles = 16, 1
     tile = rows // tiles
-    bulk_rows = (tiles - tail_tiles) * tile
 
     by_owner = emb_grad.reshape(pieces, rows, width)
     arrived, tail, sums = round_and_exchange(by_owner, mtp_grad, shards, tiles, tail_tiles)
@@ -385,9 +407,9 @@
     global_norm = jnp.sqrt(jnp.sum(group_square))
     ceiling = max_rms[0] * jnp.sqrt(jnp.float32(total_rows * model_width))
     factor = ceiling / (global_norm + 1e-06)
-    out = scale_rows(factor, arrived, None, 0, rows, tile)
+    out = scale_rows(factor, arrived, rows, tile)
     head_output = (mtp_grad * factor).astype(jnp.bfloat16)
-    out = scale_rows(factor, tail_arrived, out, bulk_rows, rows, tile)
+    out = scale_tail(factor, tail_arrived, out, tile // 4)
     return (out, head_output, group_rms)
 
 

time: 652 us -> 649 us (level)
  no operation moved by 1% of the time
where the time goes in v3:
time: 649 us; the launch traced here: 647 us
  Pallas kernels  626 us (96%)
  other arithmetic  9.72 us (1%)
    pallas_call x1, Pallas kernels, round_and_exchange(): pl.pallas_call(functools.partial(exchange_kernel, pieces, shards, tiles,...  599 us
    pallas_call x1, Pallas kernels, scale_rows(): pl.pallas_call(scale_kernel, grid=(count // tile,), in_specs=[pl.BlockSpe...  25.4 us
  transfers between devices with their start and end apart: 1, of which 1 were waited for; matrix products, arithmetic and copies ran while one was open for 2% of the time, Pallas kernels for 4%

profile of v3, /device:TPU:0, one launch (start us, length us, event | category | flops | bytes accessed | tf_op | source)
XLA Modules:
  0.0 647.5 jit_solution(9423939794391945893)
XLA Ops:
  0.6 0.0 copy-start
  0.6 0.0 copy-start.1
  0.7 599.1 %shard_map.76 = (bf16[8,1920,896]{2,1,0:T(8,128)(2,1)}, bf16[8,128,896]{2,1,0:T(8,128)(2,1)}, f32[4,8,128]{2,1,0:T(8,128)}) custom-call(f32[8,2048,896]{2,1,0:T(8,128)} %bitcast.7, f32[3584,896]{1,0:T(8,128)} %mtp.1), custom_call_target="tpu_custom_call" | custom-call | flops 44040192 | bytes 117440512 | tf_op jit(solution)/shard_map/pallas_call | solution.py:278
  599.8 3.6 all-to-all-start
  603.4 0.7 copy.11
  604.1 0.1 slice.9
  604.9 0.1 mul.46
  604.9 0.1 mul.49
  605.0 0.0 copy-done
  605.0 0.1 convert_reduce_fusion.1
  605.1 0.0 copy-done.1
  605.1 0.1 convert_reduce_fusion
  605.2 1.1 fusion
  607.1 25.4 %shard_map.77._ = bf16[2048,7168]{1,0:T(8,128)(2,1)} custom-call(f32[1]{0:T(128)} %bitcast.2.factor_ref, bf16[8,1920,896]{2,1,0:T(8,128)(2,1)} %get-tuple-element.8.x_ref), custom_call_target="tpu_custom_call" | custom-call | flops 13762560 | bytes 55050240 | tf_op jit(solution)/shard_map/pallas_call | solution.py:332
  632.5 8.4 %multiply_convert_fusion = bf16[3584,896]{1,0:T(8,128)(2,1)} fusion(f32[3584,896]{1,0:T(8,128)} %mtp.1, f32[]{:T(128)} %div.6), kind=kLoop, calls=%fused_computation | loop fusion | flops 6422528 | bytes 19267588 | tf_op jit(solution)/shard_map/convert_element_type | solution.py:411
  640.9 4.8 all-to-all-done.x_ref
  645.6 1.8 shard_map.78
  (1 shorter events, 0.0 us)
Async XLA Ops:
  0.6 604.4 %copy-start = (s32[64]{0:T(128)S(1)}, s32[64]{0:T(128)}, u32[]{:S(2)}) copy-start(s32[64]{0:T(128)} %param.7) | copy-start | bytes 772
  0.6 604.5 %copy-start.1 = (s32[32]{0:T(128)S(1)}, s32[32]{0:T(128)}, u32[]{:S(2)}) copy-start(s32[32]{0:T(128)} %param.8) | copy-start | bytes 388
  599.8 45.9 %all-to-all-start = ((bf16[8,128,896]{2,1,0:T(8,128)(2,1)}), bf16[8,128,896]{2,1,0:T(8,128)(2,1)S(1)}, u32[]{:S(2)}, u32[]{:S(2)}) async-start(bf16[8,128,896]{2,1,0:T(8,128)(2,1)} %get-tuple-element.7), calls=%async_computation | async-start | bytes 3670016 | tf_op jit(solution)/shard_map/all_to_all | solution.py:392

commit v4 on v3

--- a/solution.py
+++ b/solution.py
@@ -13,6 +13,8 @@
 STRIP = 32
 SLOTS = 6
 LEAD = 2
+TILES = 16
+TAIL_TILES = 4
 LANES = 128
 MESH = pl.DeviceIdType.MESH
 
@@ -29,7 +31,7 @@
 def exchange_kernel(
     pieces, shards, tiles, tail_tiles,
     emb, mtp, arrived, tail_out, sums,
-    low, tail, slots, head_slots, squares, mine, column_sums, shard_mine, shard_sums,
+    low, slots, head_slots, squares, mine, column_sums, shard_mine, shard_sums,
     load_sem, head_sem, send_sem, recv_sem, own_sem, tail_sem,
     stat_send, stat_recv, shard_send, shard_recv,
 ):
@@ -38,7 +40,11 @@
     tile = slots.shape[1]
     embed_blocks = pieces * rows // EMB_BLK
     head_blocks = mtp.shape[0] // MTP_BLK
+    middle = pieces // 2
     bulk = tiles - tail_tiles
+
+    def sent(k):
+        return bulk if k == middle else tiles
 
     barrier = pltpu.get_barrier_semaphore()
     for k in range(1, pieces):
@@ -108,7 +114,6 @@
             device_id_type=MESH,
         )
 
-    middle = pieces // 2
     near = list(range(2, middle))
     early = list(range(pieces - 1, middle + middle // 2 - 1, -1))
     late = list(range(middle + middle // 2 - 1, middle - 1, -1))
@@ -140,7 +145,7 @@
     for k in near + early + late + [1]:
         started = lead if k in near[:paired] + early[:paired] else 0
         prime, run = stream(
-            bulk - started,
+            tiles - started,
             lambda i: (partner(me, k, pieces), started + i),
             lambda i, at, value: store_low(k, started + i, at, value),
             lambda i: None,
@@ -149,14 +154,16 @@
         run()
         for copy in waiting:
             copy.start()
-        waiting = [send(k, started, bulk - started)] if k in near + early else []
+        waiting = [send(k, started, tiles - started)] if k in near + early else []
     first_late = late[0]
-    half = bulk // 2
-
-    own_at = pl.ds(0, bulk * tile)
-    own_copy = pltpu.make_async_copy(low.at[0, own_at, :], arrived.at[me, own_at, :], own_sem)
+    half = tiles // 2
+
+    own_copy = pltpu.make_async_copy(low.at[0], arrived.at[me], own_sem)
+    tail_copy = pltpu.make_async_copy(
+        low.at[middle, pl.ds(bulk * tile, tail_tiles * tile), :], tail_out, tail_sem
+    )
     prime, run = stream(
-        bulk,
+        tiles,
         lambda i: (me, i),
         lambda i, at, value: store_low(0, i, at, value),
         lambda i: None,
@@ -165,19 +172,7 @@
     run()
     send(first_late, 0, half).start()
 
-    def store_tail(i, at, value):
-        row = pl.multiple_of((i % tail_tiles) * tile + at, STRIP)
-        tail[i // tail_tiles, pl.ds(row, STRIP), :] = value
-
-    tail_copy = pltpu.make_async_copy(tail, tail_out, tail_sem)
-    prime, run = stream(
-        pieces * tail_tiles,
-        lambda i: (i // tail_tiles, bulk + i % tail_tiles),
-        store_tail,
-        lambda i: None,
-    )
-    prime()
-    run()
+    tail_copy.start()
     own_copy.start()
 
     def head_load(b):
@@ -219,11 +214,9 @@
     mine[...] = packed
     column_sums[me] = packed
 
-    tail_copy.start()
-
     for k in near:
-        send(k, 0, bulk).wait_send()
-    send(1, 0, bulk).start()
+        send(k, 0, tiles).wait_send()
+    send(1, 0, tiles).start()
 
     def stat_copy(k):
         return pltpu.make_async_remote_copy(
@@ -237,9 +230,9 @@
 
     for k in range(1, pieces):
         stat_copy(k).start()
-    send(first_late, half, bulk - half).start()
+    send(first_late, half, tiles - half).start()
     for k in late[1:]:
-        send(k, 0, bulk).start()
+        send(k, 0, sent(k)).start()
     for k in range(1, pieces):
         stat_copy(k).wait()
     packed = jnp.sum(column_sums[...], axis=0)
@@ -266,14 +259,13 @@
     tail_copy.wait()
     for k in range(1, pieces):
         if k not in near:
-            send(k, 0, bulk).wait_send()
-        send(k, 0, bulk).wait_recv()
+            send(k, 0, sent(k)).wait_send()
+        send(k, 0, sent(k)).wait_recv()
 
 
 def round_and_exchange(by_owner, mtp, shards, tiles, tail_tiles):
     pieces, rows, width = by_owner.shape
     tile = rows // tiles
-    bulk_rows, tail_rows = (tiles - tail_tiles) * tile, tail_tiles * tile
     blocks = pieces * rows // EMB_BLK + mtp.shape[0] // MTP_BLK
     return pl.pallas_call(
         functools.partial(exchange_kernel, pieces, shards, tiles, tail_tiles),
@@ -284,13 +276,12 @@
             pl.BlockSpec(memory_space=pltpu.VMEM),
         ],
         out_shape=[
-            jax.ShapeDtypeStruct((pieces, bulk_rows, width), jnp.bfloat16),
-            jax.ShapeDtypeStruct((pieces, tail_rows, width), jnp.bfloat16),
+            jax.ShapeDtypeStruct(by_owner.shape, jnp.bfloat16),
+            jax.ShapeDtypeStruct((tail_tiles * tile, width), jnp.bfloat16),
             jax.ShapeDtypeStruct((shards, 8, LANES), jnp.float32),
         ],
         scratch_shapes=[
-            pltpu.VMEM((pieces, bulk_rows, width), jnp.bfloat16),
-            pltpu.VMEM((pieces, tail_rows, width), jnp.bfloat16),
+            pltpu.VMEM(by_owner.shape, jnp.bfloat16),
             pltpu.VMEM((SLOTS, tile, width), jnp.float32),
             pltpu.VMEM((2, MTP_BLK, width), jnp.float32),
             pltpu.VMEM((blocks, 8, width), jnp.float32),
@@ -344,35 +335,36 @@
     )(factor.reshape(1), arrived)
 
 
-def scale_tail_kernel(step, factor_ref, x_ref, _, out_ref):
-    pieces, _, width = x_ref.shape
-    factor = factor_ref[0]
+def scale_tail_kernel(step, _, factor_ref, x_ref, __, out_ref):
     at = pl.ds(pl.multiple_of(pl.program_id(0) * step, step), step)
-    for j in range(pieces):
-        out_ref[:, j * width : (j + 1) * width] = (
-            x_ref[j, at, :].astype(jnp.float32) * factor
-        ).astype(jnp.bfloat16)
-
-
-def scale_tail(factor, arrived, out, step):
-    pieces, count, width = arrived.shape
+    out_ref[...] = (x_ref[at, :].astype(jnp.float32) * factor_ref[0]).astype(jnp.bfloat16)
+
+
+def scale_tail(factor, piece, arrived, out, step):
+    count, width = arrived.shape
     start = (out.shape[0] - count) // step
+    if width % LANES:
+        scaled = (arrived.astype(jnp.float32) * factor).astype(jnp.bfloat16)
+        return lax.dynamic_update_slice(out, scaled, (out.shape[0] - count, piece * width))
     return pl.pallas_call(
         functools.partial(scale_tail_kernel, step),
-        grid=(count // step,),
-        in_specs=[
-            pl.BlockSpec(memory_space=pltpu.SMEM),
-            pl.BlockSpec(memory_space=pltpu.VMEM),
-            pl.BlockSpec(memory_space=pl.ANY),
-        ],
-        out_specs=pl.BlockSpec((step, pieces * width), lambda i: (start + i, 0)),
+        grid_spec=pltpu.PrefetchScalarGridSpec(
+            num_scalar_prefetch=1,
+            grid=(count // step,),
+            in_specs=[
+                pl.BlockSpec(memory_space=pltpu.SMEM),
+                pl.BlockSpec(memory_space=pltpu.VMEM),
+                pl.BlockSpec(memory_space=pl.ANY),
+            ],
+            out_specs=pl.BlockSpec((step, width), lambda i, piece: (start + i, piece[0])),
+        ),
         out_shape=jax.ShapeDtypeStruct(out.shape, jnp.bfloat16),
-        input_output_aliases={2: 0},
-        compiler_params=pltpu.CompilerParams(vmem_limit_bytes=16 * step * pieces * width),
+        input_output_aliases={3: 0},
+        compiler_params=pltpu.CompilerParams(vmem_limit_bytes=32 * step * width),
         cost_estimate=pl.CostEstimate(
             flops=arrived.size, bytes_accessed=4 * arrived.size, transcendentals=0
         ),
-    )(factor.reshape(1), arrived, out)
+    )(piece.reshape(1), factor.reshape(1), arrived, out)
 
 
 def membership(labels):
@@ -384,12 +376,14 @@
     model_width = width * pieces
     total_rows = (emb_grad.shape[0] + mtp_grad.shape[0]) * shards
     rows = emb_grad.shape[0] // pieces
-    tiles, tail_tiles = 16, 1
+    tiles, tail_tiles = TILES, TAIL_TILES
     tile = rows // tiles
 
     by_owner = emb_grad.reshape(pieces, rows, width)
     arrived, tail, sums = round_and_exchange(by_owner, mtp_grad, shards, tiles, tail_tiles)
-    tail_arrived = lax.all_to_all(tail, "mp", split_axis=0, concat_axis=0, tiled=True)
+    middle = pieces // 2
+    tail_arrived = lax.ppermute(tail, "mp", [(i, (i + middle) % pieces) for i in range(pieces)])
+    source = (lax.axis_index("mp") + middle) % pieces
 
     embed_count = emb_grad.shape[0] // EMB_BLK
     head_count = mtp_grad.shape[0] // MTP_BLK
@@ -409,7 +403,7 @@
     factor = ceiling / (global_norm + 1e-06)
     out = scale_rows(factor, arrived, rows, tile)
     head_output = (mtp_grad * factor).astype(jnp.bfloat16)
-    out = scale_tail(factor, tail_arrived, out, tile // 4)
+    out = scale_tail(factor, source, tail_arrived, out, tile)
     return (out, head_output, group_rms)
 
 

time: 649 us -> 644 us (level)
  no operation moved by 1% of the time
where the time goes in v4:
time: 644 us; the launch traced here: 643 us
  Pallas kernels  627 us (97%)
  other arithmetic  9.73 us (2%)
    pallas_call x1, Pallas kernels, round_and_exchange(): pl.pallas_call(functools.partial(exchange_kernel, pieces, shards, tiles,...  599 us
    pallas_call x1, Pallas kernels, scale_rows(): pl.pallas_call(scale_kernel, grid=(count // tile,), in_specs=[pl.BlockSpe...  26 us
  transfers between devices with their start and end apart: 1, of which 1 were waited for; matrix products, arithmetic and copies ran while one was open for 2% of the time, Pallas kernels for 4%

profile of v4, /device:TPU:0, one launch (start us, length us, event | category | flops | bytes accessed | tf_op | source)
XLA Modules:
  0.0 642.8 jit_solution(3341124262024696669)
XLA Ops:
  0.6 0.0 copy-start
  0.6 0.0 copy-start.1
  0.7 599.1 %shard_map.76 = (bf16[8,2048,896]{2,1,0:T(8,128)(2,1)}, bf16[512,896]{1,0:T(8,128)(2,1)}, f32[4,8,128]{2,1,0:T(8,128)}) custom-call(f32[8,2048,896]{2,1,0:T(8,128)} %bitcast.8, f32[3584,896]{1,0:T(8,128)} %mtp.1), custom_call_target="tpu_custom_call" | custom-call | flops 44040192 | bytes 117440512 | tf_op jit(solution)/shard_map/pallas_call | solution.py:270
  599.8 0.1 collective-permute-start
  599.9 0.7 copy.11
  600.6 0.1 slice.9
  601.3 0.1 mul.46
  601.4 0.1 mul.49
  601.5 0.0 copy-done
  601.5 0.1 convert_reduce_fusion
  601.6 0.0 copy-done.1
  601.6 0.1 convert_reduce_fusion.1
  601.7 1.1 fusion
  603.6 26.0 %shard_map.77.__ = bf16[2048,7168]{1,0:T(8,128)(2,1)} custom-call(f32[1]{0:T(128)} %bitcast.3.factor_ref, bf16[8,2048,896]{2,1,0:T(8,128)(2,1)} %get-tuple-element.8.x_ref), custom_call_target="tpu_custom_call" | custom-call | flops 14680064 | bytes 58720256 | tf_op jit(solution)/shard_map/pallas_call | solution.py:323
  629.6 8.4 %multiply_convert_fusion = bf16[3584,896]{1,0:T(8,128)(2,1)} fusion(f32[3584,896]{1,0:T(8,128)} %mtp.1, f32[]{:T(128)} %div.6), kind=kLoop, calls=%fused_computation | loop fusion | flops 6422528 | bytes 19267588 | tf_op jit(solution)/shard_map/convert_element_type | solution.py:405
  638.0 3.2 collective-permute-done.x_ref
  641.2 1.5 shard_map.78
  (1 shorter events, 0.0 us)
Async XLA Ops:
  0.6 600.9 %copy-start = (s32[32]{0:T(128)S(1)}, s32[32]{0:T(128)}, u32[]{:S(2)}) copy-start(s32[32]{0:T(128)} %param.8) | copy-start | bytes 388
  0.6 601.0 %copy-start.1 = (s32[64]{0:T(128)S(1)}, s32[64]{0:T(128)}, u32[]{:S(2)}) copy-start(s32[64]{0:T(128)} %param.7) | copy-start | bytes 772
  599.8 41.4 %collective-permute-start = (bf16[512,896]{1,0:T(8,128)(2,1)}, bf16[512,896]{1,0:T(8,128)(2,1)S(1)}, u32[]{:S(2)}, u32[]{:S(2)}) collective-permute-start(bf16[512,896]{1,0:T(8,128)(2,1)} %get-tuple-element.7), channel_id=1, source_target_pairs={{0,4},{1,5},{2,6},{3,7},{4,0},{5,1},{6,2},{7,3},{8,12},{9,13},{10,... | collective-permute-start | bytes 2752520 | tf_op jit(solution)/shard_map/ppermute | solution.py:385

commit v5 on v4

--- a/solution.py
+++ b/solution.py
@@ -41,10 +41,11 @@
     embed_blocks = pieces * rows // EMB_BLK
     head_blocks = mtp.shape[0] // MTP_BLK
     middle = pieces // 2
+    held = pieces - 2
     bulk = tiles - tail_tiles
 
     def sent(k):
-        return bulk if k == middle else tiles
+        return bulk if k == held else tiles
 
     barrier = pltpu.get_barrier_semaphore()
     for k in range(1, pieces):
@@ -114,15 +115,16 @@
             device_id_type=MESH,
         )
 
-    near = list(range(2, middle))
-    early = list(range(pieces - 1, middle + middle // 2 - 1, -1))
+    near = list(range(middle - 1, 1, -1))
+    early = [held, pieces - 1] + list(range(middle + middle // 2, held))
     late = list(range(middle + middle // 2 - 1, middle - 1, -1))
     lead = min(LEAD, bulk - 1)
-    paired = min(len(near), len(early))
+    paired = 2
 
     def lead_piece(i):
         pair = (i // 2) % paired
-        return (1 - i % 2) * (2 + pair) + (i % 2) * (pieces - 1 - pair)
+        near_piece, early_piece = middle - 1 - pair, held + pair
+        return (1 - i % 2) * near_piece + (i % 2) * early_piece
 
     def lead_tile(i):
         return i // (2 * paired)
@@ -141,7 +143,9 @@
         send(near[pair], 0, lead).start()
         send(early[pair], 0, lead).start()
 
-    waiting = []
+    inner = ((me // (pieces // 4) + 1) // 2) % 2
+    split_send = send(near[0], bulk, tiles - bulk)
+    waiting, waiting_split = [], False
     for k in near + early + late + [1]:
         started = lead if k in near[:paired] + early[:paired] else 0
         prime, run = stream(
@@ -154,13 +158,27 @@
         run()
         for copy in waiting:
             copy.start()
-        waiting = [send(k, started, tiles - started)] if k in near + early else []
+        if waiting_split:
+            waiting_split = False
+
+            @pl.when(inner == 0)
+            def _():
+                split_send.start()
+
+        if k == near[-1]:
+            waiting = [send(k, started, tiles - started)]
+            waiting_split = True
+        elif k in near + early:
+            stop = bulk if k in (near[0], held) else tiles
+            waiting = [send(k, started, stop - started)]
+        else:
+            waiting = []
     first_late = late[0]
     half = tiles // 2
 
     own_copy = pltpu.make_async_copy(low.at[0], arrived.at[me], own_sem)
     tail_copy = pltpu.make_async_copy(
-        low.at[middle, pl.ds(bulk * tile, tail_tiles * tile), :], tail_out, tail_sem
+        low.at[held, pl.ds(bulk * tile, tail_tiles * tile), :], tail_out, tail_sem
     )
     prime, run = stream(
         tiles,
@@ -214,9 +232,13 @@
     mine[...] = packed
     column_sums[me] = packed
 
-    for k in near:
+    for k in near[1:]:
         send(k, 0, tiles).wait_send()
     send(1, 0, tiles).start()
+
+    @pl.when(inner == 1)
+    def _():
+        split_send.start()
 
     def stat_copy(k):
         return pltpu.make_async_remote_copy(
@@ -258,7 +280,7 @@
     own_copy.wait()
     tail_copy.wait()
     for k in range(1, pieces):
-        if k not in near:
+        if k not in near[1:]:
             send(k, 0, sent(k)).wait_send()
         send(k, 0, sent(k)).wait_recv()
 
@@ -381,9 +403,10 @@
 
     by_owner = emb_grad.reshape(pieces, rows, width)
     arrived, tail, sums = round_and_exchange(by_owner, mtp_grad, shards, tiles, tail_tiles)
-    middle = pieces // 2
-    tail_arrived = lax.ppermute(tail, "mp", [(i, (i + middle) % pieces) for i in range(pieces)])
-    source = (lax.axis_index("mp") + middle) % pieces
+    held = pieces - 2
+    pairs = [(i, partner(i, held, pieces)) for i in range(pieces)]
+    tail_arrived = lax.ppermute(tail, "mp", pairs)
+    source = partner(lax.axis_index("mp"), held, pieces)
 
     embed_count = emb_grad.shape[0] // EMB_BLK
     head_count = mtp_grad.shape[0] // MTP_BLK
@@ -401,9 +424,9 @@
     global_norm = jnp.sqrt(jnp.sum(group_square))
     ceiling = max_rms[0] * jnp.sqrt(jnp.float32(total_rows * model_width))
     factor = ceiling / (global_norm + 1e-06)
-    out = scale_rows(factor, arrived, rows, tile)
+    out = scale_rows(factor, arrived, rows, 2 * tile)
     head_output = (mtp_grad * factor).astype(jnp.bfloat16)
-    out = scale_tail(factor, source, tail_arrived, out, tile)
+    out = scale_tail(factor, source, tail_arrived, out, 2 * tile)
     return (out, head_output, group_rms)
 
 

time: 644 us -> 640 us (level)
  transfers between devices with their start and end apart: 1 -> 1, of which waited for: 1 -> 0; matrix products, arithmetic and copies ran while one was open for 2% -> 2% of each run, Pallas kernels for 4% -> 3%
where the time goes in v5:
time: 640 us; the launch traced here: 637 us
  Pallas kernels  623 us (97%)
  other arithmetic  9.73 us (2%)
    pallas_call x1, Pallas kernels, round_and_exchange(): pl.pallas_call(functools.partial(exchange_kernel, pieces, shards, tiles,...  600 us
    pallas_call x1, Pallas kernels, scale_rows(): pl.pallas_call(scale_kernel, grid=(count // tile,), in_specs=[pl.BlockSpe...  21.8 us
  transfers between devices with their start and end apart: 1, of which 0 were waited for; matrix products, arithmetic and copies ran while one was open for 2% of the time, Pallas kernels for 3%

profile of v5, /device:TPU:0, one launch (start us, length us, event | category | flops | bytes accessed | tf_op | source)
XLA Modules:
  0.0 637.4 jit_solution(14476958115163239152)
XLA Ops:
  0.6 0.0 copy-start
  0.6 0.0 copy-start.1
  0.7 599.8 %shard_map.76 = (bf16[8,2048,896]{2,1,0:T(8,128)(2,1)}, bf16[512,896]{1,0:T(8,128)(2,1)}, f32[4,8,128]{2,1,0:T(8,128)}) custom-call(f32[8,2048,896]{2,1,0:T(8,128)} %bitcast.8, f32[3584,896]{1,0:T(8,128)} %mtp.1), custom_call_target="tpu_custom_call" | custom-call | flops 44040192 | bytes 117440512 | tf_op jit(solution)/shard_map/pallas_call | solution.py:292
  600.5 2.0 collective-permute-start
  602.4 0.7 copy.11
  603.2 0.1 slice.9
  603.9 0.1 mul.62
  604.0 0.1 mul.65
  604.1 0.0 copy-done
  604.1 0.1 convert_reduce_fusion
  604.2 0.0 copy-done.1
  604.2 0.1 convert_reduce_fusion.1
  604.3 1.1 fusion
  606.2 21.8 %shard_map.77.__ = bf16[2048,7168]{1,0:T(8,128)(2,1)} custom-call(f32[1]{0:T(128)} %bitcast.3.factor_ref, bf16[8,2048,896]{2,1,0:T(8,128)(2,1)} %get-tuple-element.8.x_ref), custom_call_target="tpu_custom_call" | custom-call | flops 14680064 | bytes 58720256 | tf_op jit(solution)/shard_map/pallas_call | solution.py:345
  628.0 8.4 %multiply_convert_fusion = bf16[3584,896]{1,0:T(8,128)(2,1)} fusion(f32[3584,896]{1,0:T(8,128)} %mtp.1, f32[]{:T(128)} %div.28), kind=kLoop, calls=%fused_computation | loop fusion | flops 6422528 | bytes 19267588 | tf_op jit(solution)/shard_map/convert_element_type | solution.py:428
  636.4 0.0 collective-permute-done.x_ref
  636.4 1.0 shard_map.78
  (1 shorter events, 0.0 us)
Async XLA Ops:
  0.6 603.4 %copy-start = (s32[32]{0:T(128)S(1)}, s32[32]{0:T(128)}, u32[]{:S(2)}) copy-start(s32[32]{0:T(128)} %param.8) | copy-start | bytes 388
  0.6 603.5 %copy-start.1 = (s32[64]{0:T(128)S(1)}, s32[64]{0:T(128)}, u32[]{:S(2)}) copy-start(s32[64]{0:T(128)} %param.7) | copy-start | bytes 772
  600.5 35.9 %collective-permute-start = (bf16[512,896]{1,0:T(8,128)(2,1)}, bf16[512,896]{1,0:T(8,128)(2,1)S(1)}, u32[]{:S(2)}, u32[]{:S(2)}) collective-permute-start(bf16[512,896]{1,0:T(8,128)(2,1)} %get-tuple-element.7), channel_id=1, source_target_pairs={{0,6},{1,7},{2,4},{3,5},{4,2},{5,3},{6,0},{7,1},{8,14},{9,15},{10,... | collective-permute-start | bytes 2752520 | tf_op jit(solution)/shard_map/ppermute | solution.py:408
